TPU v7x, 256 devices: a whole 4x4x8 slice. The times are simulated.
256 devices in a mesh: gx: 8 (over y, core), gy: 16 (over z, x_lo), gz: 2 (over x_hi).
Axes of the slice: x: 4 (x_hi: 2, x_lo: 2; x = x_hi * 2 + x_lo), y: 4, z: 8, core: 2. Of those that a mesh axis runs over, the one named last changes fastest.
Arguments:
- directions: float32 [8, 128, 256, 256], P(None, 'gx', 'gy', 'gz'), may hold values from -6 to 6
- state: float32 [128, 256, 256], P('gx', 'gy', 'gz'), may hold values from -2 to 2
- log_cond: float32 [128, 256, 256], P('gx', 'gy', 'gz'), may hold values from -1 to 1
- obs_mask: int32 [128, 256, 256], P('gx', 'gy', 'gz'), may hold values 0 or 1
Outputs:
- hessian_action: float32 [8, 128, 256, 256], P(None, 'gx', 'gy', 'gz')
- quotient: float32 [8], replicated
All inputs are finite; a program needn't handle non-finite values. No bound on the sum of `obs_mask` on one device may be relied on, other than what follows from the above.
Results may differ from a plain program's by a relative error of at most 0.00002.
Values sent between devices are 32-bit elements; how exact they have to be, the bound alone decides.
A program may use at most 128 MiB of HBM per device.

v0:
```python
import math
import jax
import jax.numpy as jnp
from jax import lax
from jax.sharding import Mesh
from jax.sharding import PartitionSpec as P

ITERS = 4
GX_GY_GZ = ("gx_0", "gx_1", "gy_0", "gy_1", "gz")
GX = ("gx_0", "gx_1")
GY = ("gy_0", "gy_1")
SHIFT = 0.3
BETA = 0.05
DATA_WEIGHT = 10.0


def with_halo(shard, sides, width):
    for axis, dim in sides:
        size, length = (lax.axis_size(axis), shard.shape[dim])
        up = [(i, (i + 1) % size) for i in range(size - 1)]
        down = [(j, i) for i, j in up]
        last = lax.slice_in_dim(shard, length - width, length, axis=dim)
        leading = lax.slice_in_dim(shard, 0, width, axis=dim)
        before = lax.ppermute(last, axis, up)
        after = lax.ppermute(leading, axis, down)
        shard = jnp.concatenate([before, shard, after], axis=dim)
    return shard


def over_axes(shard, axes):
    for axis in axes:
        shard = lax.psum(shard, axis)
    return shard


def chebyshev(count):
    return [
        1.0 / (1.125 + 0.825 * math.cos(math.pi * (2 * j + 1) / (2 * count))) for j in range(count)
    ]


def neighbours(padded):
    total = padded[..., 2:, 1:-1, 1:-1] + padded[..., :-2, 1:-1, 1:-1]
    total = total + padded[..., 1:-1, 2:, 1:-1] + padded[..., 1:-1, :-2, 1:-1]
    return total + padded[..., 1:-1, 1:-1, 2:] + padded[..., 1:-1, 1:-1, :-2]


def trim_rim(field, layers):
    return field[..., layers:-layers, layers:-layers, layers:-layers]


def trim_to(field, layers):
    if layers == 0:
        return field
    return trim_rim(field, layers)


def shards(directions, state, log_cond, obs_mask):
    cheb_w = chebyshev(ITERS)
    conduct = jnp.exp(log_cond)
    observed = obs_mask.astype(jnp.float32)
    outer = ITERS - 1
    stacked = jnp.concatenate([state[None], conduct[None], directions], axis=0)
    padded = with_halo(stacked, ((GX, 1), (GY, 2), ("gz", 3)), ITERS)
    state_wide = padded[0]
    conduct_wide = trim_rim(padded[1], 1)
    diagonal_wide = SHIFT + 6.0 * conduct_wide
    delta_wide = padded[2:]
    lap_wide = 6.0 * trim_rim(state_wide, 1) - neighbours(state_wide)
    source_wide = -conduct_wide * trim_rim(delta_wide, 1) * lap_wide
    tangent = cheb_w[0] * source_wide / diagonal_wide
    margin = outer
    for step in range(1, ITERS):
        margin = margin - 1
        cut = outer - margin
        inner = trim_rim(tangent, 1)
        cond_here = trim_to(conduct_wide, cut)
        diag_here = trim_to(diagonal_wide, cut)
        applied = diag_here * inner - cond_here * neighbours(tangent)
        tangent = inner + cheb_w[step] * (trim_to(source_wide, cut) - applied) / diag_here
    data_rhs = DATA_WEIGHT * observed * tangent
    rhs_wide = with_halo(data_rhs, ((GX, 1), (GY, 2), ("gz", 3)), outer)
    adjoint = cheb_w[0] * rhs_wide / diagonal_wide
    margin = outer
    for step in range(1, ITERS):
        flux = trim_to(conduct_wide, outer - margin) * adjoint
        margin = margin - 1
        cut = outer - margin
        inner = trim_rim(adjoint, 1)
        diag_here = trim_to(diagonal_wide, cut)
        applied = diag_here * inner - neighbours(flux)
        adjoint = inner + cheb_w[step] * (trim_to(rhs_wide, cut) - applied) / diag_here
    lap_state = trim_to(lap_wide, outer)
    delta_pad = trim_to(delta_wide, outer)
    hessian_action = -conduct * lap_state * adjoint + BETA * (
        6.0 * directions - neighbours(delta_pad)
    )
    cells = (
        directions.shape[1]
        * directions.shape[2]
        * directions.shape[3]
        * lax.axis_size(GX)
        * lax.axis_size(GY)
        * lax.axis_size("gz")
    )
    partial_sums = jnp.sum(directions * hessian_action, axis=(1, 2, 3))
    quotient = over_axes(partial_sums, GX_GY_GZ) / cells
    return (hessian_action, quotient)


def solution(mesh):
    torus = Mesh(
        mesh.devices.reshape(4, 2, 8, 2, mesh.shape["gz"]), ("gx_0", "gx_1", "gy_0", "gy_1", "gz")
    )
    placed = (P(None, GX, GY, "gz"), P(GX, GY, "gz"), P(GX, GY, "gz"), P(GX, GY, "gz"))
    return jax.shard_map(
        shards, mesh=torus, in_specs=placed, out_specs=(P(None, GX, GY, "gz"), P()), check_vma=False
    )
```

profile of v0, /device:TPU:6, one launch (start us, length us, event | category | flops | bytes accessed | tf_op | source)
XLA Modules:
  0.0 248.0 jit_solution(18383695558841984095)
XLA Ops:
  6.0 3.5 %collective-permute-done.1 = f32[10,4,16,128]{3,2,1,0:T(8,128)S(1)} collective-permute-done((f32[10,4,16,128]{3,2,1,0:T(8,128)S(1)}, f32[10,4,16,128]{3,2,1,0:T(8,128)S(1)}, u32[]{:S(2)}, u32[]{:S(2)}) %collective-permute-start.1) | collective-permute-done | bytes 327712 | tf_op jit(solution)/shard_map/ppermute | solution.py:25
  13.9 4.0 %collective-permute-start.2 = (f32[10,24,4,128]{3,1,2,0:T(8,128)S(1)}, f32[10,24,4,128]{3,1,2,0:T(8,128)S(1)}, u32[]{:S(2)}, u32[]{:S(2)}) collective-permute-start(f32[10,24,4,128]{3,1,2,0:T(8,128)S(1)} %copy.39), channel_id=1, source_target_pairs={{0,2},{2,4},{4,6},{6,8},{8,10},{10,12},{12,14},{14,16},{16,18},{18... | collective-permute-start | bytes 1474568 | tf_op jit(solution)/shard_map/ppermute | solution.py:24
  17.9 5.8 %collective-permute-done.3 = f32[10,24,4,128]{3,1,2,0:T(8,128)S(1)} collective-permute-done((f32[10,24,4,128]{3,1,2,0:T(8,128)S(1)}, f32[10,24,4,128]{3,1,2,0:T(8,128)S(1)}, u32[]{:S(2)}, u32[]{:S(2)}) %collective-permute-start.3) | collective-permute-done | bytes 491552 | tf_op jit(solution)/shard_map/ppermute | solution.py:25
  23.9 14.6 %collective-permute-done.2 = f32[10,24,4,128]{3,1,2,0:T(8,128)S(1)} collective-permute-done((f32[10,24,4,128]{3,1,2,0:T(8,128)S(1)}, f32[10,24,4,128]{3,1,2,0:T(8,128)S(1)}, u32[]{:S(2)}, u32[]{:S(2)}) %collective-permute-start.2) | collective-permute-done | bytes 491552 | tf_op jit(solution)/shard_map/ppermute | solution.py:24
  42.5 3.7 %copy.44 = f32[10,24,24,4]{2,1,3,0:T(8,128)} copy(f32[10,24,24,4]{3,2,1,0:T(8,128)} %get-tuple-element.17) | data formatting | bytes 184320 | tf_op jit(solution)/shard_map/slice | solution.py:23
  49.9 7.9 %collective-permute-start.5 = (f32[10,24,24,4]{2,1,3,0:T(8,128)}, f32[10,24,24,4]{2,1,3,0:T(8,128)}, u32[]{:S(2)}, u32[]{:S(2)}) collective-permute-start(f32[10,24,24,4]{2,1,3,0:T(8,128)} %copy.44), channel_id=1, source_target_pairs={{1,0},{3,2},{5,4},{7,6},{9,8},{11,10},{13,12},{15,14},{17,16},{19,... | collective-permute-start | bytes 276488 | tf_op jit(solution)/shard_map/ppermute | solution.py:25
  59.4 8.2 %collective-permute-done.5 = f32[10,24,24,4]{2,1,3,0:T(8,128)} collective-permute-done((f32[10,24,24,4]{2,1,3,0:T(8,128)}, f32[10,24,24,4]{2,1,3,0:T(8,128)}, u32[]{:S(2)}, u32[]{:S(2)}) %collective-permute-start.5) | collective-permute-done | bytes 92192 | tf_op jit(solution)/shard_map/ppermute | solution.py:25
  70.1 3.9 %copy.45 = f32[10,24,24,4]{3,2,1,0:T(8,128)} copy(f32[10,24,24,4]{2,1,3,0:T(8,128)} %collective-permute-done.4) | data formatting | bytes 184320 | tf_op jit(solution)/shard_map/ppermute | solution.py:24
  74.0 8.5 %pad_maximum_fusion = f32[10,24,24,136]{3,2,1,0:T(8,128)S(1)} fusion(f32[10,24,24,4]{3,2,1,0:T(8,128)S(1)} %copy.46, f32[10,24,4,128]{3,2,1,0:T(4,128)S(1)} %copy.42, f32[10,4,16,128]{3,2,1,0:T(8,128)} %copy-done.12, f32[8,16,16,128]{3,2,1,0:T(8,128)} %param.4, f32[1,16,16,128]{3,2,1,0:T(8,128)} %copy-done.14, f32[1,16,16,128]{3,2,1,0:T(8,128)} %bitcast.9, ...), kind=kLoop, calls=%fused_computation | loop fusion | flops 6266880 | bytes 6266880 | tf_op jit(solution)/shard_map/concatenate | solution.py:26
  87.0 7.5 %fusion.11 = f32[8,20,20,132]{3,2,1,0:T(8,128)S(1)} fusion(f32[8,22,22,134]{3,2,1,0:T(8,128)S(1)} %get-tuple-element.13, f32[8,22,22,134]{3,2,1,0:T(8,128)S(1)} %get-tuple-element.14, f32[20,20,132]{2,1,0:T(8,128)S(1)} %slice.379, f32[20,20,132]{2,1,0:T(8,128)S(1)} %slice.378), kind=kLoop, calls=%fused_computation.26 | loop fusion | flops 5068800 | bytes 15628800 | tf_op jit(solution)/shard_map/add | solution.py:80
  94.5 7.3 %fusion.22 = f32[8,18,18,130]{3,2,1,0:T(8,128)S(1)} fusion(f32[8,20,20,132]{3,2,1,0:T(8,128)S(1)} %fusion.11, f32[8,22,22,134]{3,2,1,0:T(8,128)S(1)} %get-tuple-element.14, f32[18,18,130]{2,1,0:T(8,128)S(1)} %slice.389, f32[18,18,130]{2,1,0:T(8,128)S(1)} %slice.388), kind=kLoop, calls=%fused_computation.47 | loop fusion | flops 4043520 | bytes 12467520 | tf_op jit(solution)/shard_map/add | solution.py:80
  108.6 7.4 %collective-permute-done.7 = f32[8,3,16,128]{3,2,1,0:T(8,128)S(1)} collective-permute-done((f32[8,3,16,128]{3,2,1,0:T(8,128)S(1)}, f32[8,3,16,128]{3,2,1,0:T(8,128)S(1)}, u32[]{:S(2)}, u32[]{:S(2)}) %collective-permute-start.7) | collective-permute-done | bytes 196640 | tf_op jit(solution)/shard_map/ppermute | solution.py:25
  119.4 4.8 %collective-permute-start.8 = (f32[8,22,3,128]{3,0,2,1:T(8,128)S(1)}, f32[8,22,3,128]{3,0,2,1:T(8,128)S(1)}, u32[]{:S(2)}, u32[]{:S(2)}) collective-permute-start(f32[8,22,3,128]{3,0,2,1:T(8,128)S(1)} %copy.47), channel_id=1, source_target_pairs={{0,2},{2,4},{4,6},{6,8},{8,10},{10,12},{12,14},{14,16},{16,18},{18... | collective-permute-start | bytes 811016 | tf_op jit(solution)/shard_map/ppermute | solution.py:24
  126.9 8.2 %collective-permute-done.8 = f32[8,22,3,128]{3,0,2,1:T(8,128)S(1)} collective-permute-done((f32[8,22,3,128]{3,0,2,1:T(8,128)S(1)}, f32[8,22,3,128]{3,0,2,1:T(8,128)S(1)}, u32[]{:S(2)}, u32[]{:S(2)}) %collective-permute-start.8) | collective-permute-done | bytes 270368 | tf_op jit(solution)/shard_map/ppermute | solution.py:24
  143.0 5.9 %collective-permute-start.11 = (f32[8,22,22,3]{2,0,3,1:T(8,128)S(1)}, f32[8,22,22,3]{2,0,3,1:T(8,128)S(1)}, u32[]{:S(2)}, u32[]{:S(2)}) collective-permute-start(f32[8,22,22,3]{2,0,3,1:T(8,128)S(1)} %copy.52), channel_id=1, source_target_pairs={{1,0},{3,2},{5,4},{7,6},{9,8},{11,10},{13,12},{15,14},{17,16},{19,... | collective-permute-start | bytes 139400 | tf_op jit(solution)/shard_map/ppermute | solution.py:25
  152.0 8.8 %collective-permute-done.10 = f32[8,22,22,3]{2,0,3,1:T(8,128)S(1)} collective-permute-done((f32[8,22,22,3]{2,0,3,1:T(8,128)}, f32[8,22,22,3]{2,0,3,1:T(8,128)S(1)}, u32[]{:S(2)}, u32[]{:S(2)}) %collective-permute-start.10) | collective-permute-done | bytes 46496 | tf_op jit(solution)/shard_map/ppermute | solution.py:24
  165.8 8.1 %broadcast_multiply_fusion = (f32[8,22,22,134]{3,2,1,0:T(8,128)S(1)}, f32[8,22,22,134]{3,2,1,0:T(8,128)}, f32[8,22,22,134]{3,2,1,0:T(8,128)S(1)}) fusion(f32[22,22,134]{2,1,0:T(8,128)} %get-tuple-element.29, f32[22,22,134]{2,1,0:T(8,128)S(1)} %copy-done.5, f32[8,22,22,3]{3,2,1,0:T(8,128)} %copy.54, f32[8,22,3,128]{3,2,1,0:T(4,128)S(1)} %copy-done.25, ...), kind=kLoop, calls=%fused_computation.54 | loop fusion | flops 4669632 | bytes 8820416 | tf_op jit(solution)/shard_map/mul | solution.py:86
  173.8 10.6 %broadcast_multiply_fusion.1 = (f32[8,20,20,132]{3,2,1,0:T(8,128)S(1)}, f32[8,20,20,132]{3,2,1,0:T(8,128)}) fusion(f32[20,20,132]{2,1,0:T(8,128)S(1)} %copy-done.17, f32[8,22,22,134]{3,2,1,0:T(8,128)S(1)} %get-tuple-element.10, f32[20,20,132]{2,1,0:T(8,128)S(1)} %copy-done.19, f32[8,22,22,134]{3,2,1,0:T(8,128)S(1)} %get-tuple-element.12, ...), kind=kLoop, calls=%fused_computation.55 | loop fusion | flops 5068800 | bytes 17318400 | tf_op jit(solution)/shard_map/mul | solution.py:86
  184.5 10.3 %broadcast_multiply_fusion.2 = (f32[8,18,18,130]{3,2,1,0:T(8,128)S(1)}, f32[8,18,18,130]{3,2,1,0:T(8,128)}) fusion(f32[18,18,130]{2,1,0:T(8,128)} %copy-done.20, f32[8,20,20,132]{3,2,1,0:T(8,128)S(1)} %get-tuple-element.8, f32[18,18,130]{2,1,0:T(8,128)} %copy-done.21, f32[8,22,22,134]{3,2,1,0:T(8,128)S(1)} %get-tuple-element.12, ...), kind=kLoop, calls=%fused_computation.56 | loop fusion | flops 4043520 | bytes 13815360 | tf_op jit(solution)/shard_map/mul | solution.py:86
  194.9 7.7 %multiply_reduce_fusion = (f32[8]{0:T(128)S(1)}, f32[8,16,16,128]{3,2,1,0:T(8,128)}) fusion(f32[8,16,16,128]{3,2,1,0:T(8,128)S(1)} %copy-done.3, f32[10,24,4,128]{3,2,1,0:T(4,128)S(1)} %copy-done.7, f32[10,4,16,128]{3,2,1,0:T(8,128)S(1)} %copy-done.13, f32[1,16,16,128]{3,2,1,0:T(8,128)S(1)} %copy-done.15, f32[1,16,16,128]{3,2,1,0:T(8,128)S(1)} %bitcast.11, ...), kind=kLoop, calls=%fused_computation.117 | loop fusion | flops 13893624 | bytes 12832800 | tf_op jit(solution)/shard_map/reduce_sum | solution.py:106
  202.6 11.8 %psum.35 = f32[8]{0:T(128)S(1)} all-reduce(f32[8]{0:T(128)S(1)} %get-tuple-element.4), channel_id=1, replica_groups=mesh['gx_0'=4,'gx_1'=2,'gy_0'=8,'gy_1'=2,'gz'=2] {'gx_0'}, use_global_device_ids=true, to_apply=%region_1.0 | all-reduce | flops 8 | bytes 64 | tf_op jit(solution)/shard_map/psum | solution.py:32
  216.8 19.1 %psum.37 = f32[8]{0:T(128)S(1)} all-reduce(f32[8]{0:T(128)S(1)} %psum.36), channel_id=1, replica_groups=mesh['gx_0'=4,'gx_1'=2,'gy_0'=8,'gy_1'=2,'gz'=2] {'gy_0'}, use_global_device_ids=true, to_apply=%region_3.0 | all-reduce | flops 8 | bytes 64 | tf_op jit(solution)/shard_map/psum | solution.py:32
  235.9 4.9 %psum.38 = f32[8]{0:T(128)S(1)} all-reduce(f32[8]{0:T(128)S(1)} %psum.37), channel_id=1, replica_groups=mesh['gx_0'=4,'gx_1'=2,'gy_0'=8,'gy_1'=2,'gz'=2] {'gy_1'}, use_global_device_ids=true, to_apply=%region_4.0 | all-reduce | flops 8 | bytes 64 | tf_op jit(solution)/shard_map/psum | solution.py:32
  240.8 6.4 %psum.39 = f32[8]{0:T(128)S(1)} all-reduce(f32[8]{0:T(128)S(1)} %psum.38), channel_id=1, replica_groups=mesh['gx_0'=4,'gx_1'=2,'gy_0'=8,'gy_1'=2,'gz'=2] {'gz'}, use_global_device_ids=true, to_apply=%region_5.0 | all-reduce | flops 8 | bytes 64 | tf_op jit(solution)/shard_map/psum | solution.py:32
  (118 shorter events, 57.6 us)
Async XLA Ops:
  1.6 37.0 %copy-start.14 = (f32[1,16,16,128]{3,2,1,0:T(8,128)}, f32[1,16,16,128]{3,2,1,0:T(8,128)S(1)}, u32[]{:S(2)}) copy-start(f32[1,16,16,128]{3,2,1,0:T(8,128)S(1)} %exponential_bitcast_fusion) | copy-start | bytes 393220
  2.7 36.7 %copy-start.2 = (f32[8,16,16,128]{3,2,1,0:T(8,128)S(1)}, f32[8,16,16,128]{3,2,1,0:T(8,128)}, u32[]{:S(2)}) copy-start(f32[8,16,16,128]{3,2,1,0:T(8,128)} %param.4) | copy-start | bytes 3145732
  2.7 36.6 %copy-start.22 = (f32[16,16,128]{2,1,0:T(8,128)S(1)}, f32[16,16,128]{2,1,0:T(8,128)}, u32[]{:S(2)}) copy-start(f32[16,16,128]{2,1,0:T(8,128)} %param.5) | copy-start | bytes 393220
  2.7 3.2 %collective-permute-start = (f32[10,4,16,128]{3,2,1,0:T(8,128)S(1)}, f32[10,4,16,128]{3,2,1,0:T(8,128)S(1)}, u32[]{:S(2)}, u32[]{:S(2)}) collective-permute-start(f32[10,4,16,128]{3,2,1,0:T(8,128)S(1)} %get-tuple-element.25), channel_id=1, source_target_pairs={{0,32},{32,64},{64,96},{96,128},{128,160},{160,192},{192,224},{1,3... | collective-permute-start | bytes 983048 | tf_op jit(solution)/shard_map/ppermute | solution.py:24
  4.6 4.9 %collective-permute-start.1 = (f32[10,4,16,128]{3,2,1,0:T(8,128)S(1)}, f32[10,4,16,128]{3,2,1,0:T(8,128)S(1)}, u32[]{:S(2)}, u32[]{:S(2)}) collective-permute-start(f32[10,4,16,128]{3,2,1,0:T(8,128)S(1)} %get-tuple-element.26), channel_id=1, source_target_pairs={{32,0},{64,32},{96,64},{128,96},{160,128},{192,160},{224,192},{33,... | collective-permute-start | bytes 983048 | tf_op jit(solution)/shard_map/ppermute | solution.py:25
  5.9 33.9 %copy-start.10 = (f32[10,4,16,128]{3,2,1,0:T(8,128)}, f32[10,4,16,128]{3,2,1,0:T(8,128)S(1)}, u32[]{:S(2)}) copy-start(f32[10,4,16,128]{3,2,1,0:T(8,128)S(1)} %collective-permute-done) | copy-start | bytes 983044
  9.5 30.4 %copy-start.12 = (f32[10,4,16,128]{3,2,1,0:T(8,128)}, f32[10,4,16,128]{3,2,1,0:T(8,128)S(1)}, u32[]{:S(2)}) copy-start(f32[10,4,16,128]{3,2,1,0:T(8,128)S(1)} %collective-permute-done.1) | copy-start | bytes 983044
  11.1 12.6 %collective-permute-start.3 = (f32[10,24,4,128]{3,1,2,0:T(8,128)S(1)}, f32[10,24,4,128]{3,1,2,0:T(8,128)S(1)}, u32[]{:S(2)}, u32[]{:S(2)}) collective-permute-start(f32[10,24,4,128]{3,1,2,0:T(8,128)S(1)} %copy.40), channel_id=1, source_target_pairs={{2,0},{4,2},{6,4},{8,6},{10,8},{12,10},{14,12},{16,14},{18,16},{20... | collective-permute-start | bytes 1474568 | tf_op jit(solution)/shard_map/ppermute | solution.py:25
  13.9 24.5 %collective-permute-start.2 = (f32[10,24,4,128]{3,1,2,0:T(8,128)S(1)}, f32[10,24,4,128]{3,1,2,0:T(8,128)S(1)}, u32[]{:S(2)}, u32[]{:S(2)}) collective-permute-start(f32[10,24,4,128]{3,1,2,0:T(8,128)S(1)} %copy.39), channel_id=1, source_target_pairs={{0,2},{2,4},{4,6},{6,8},{8,10},{10,12},{12,14},{14,16},{16,18},{18... | collective-permute-start | bytes 1474568 | tf_op jit(solution)/shard_map/ppermute | solution.py:24
  23.9 50.2 %copy-start.6 = (f32[10,24,4,128]{3,2,1,0:T(4,128)}, f32[10,24,4,128]{3,2,1,0:T(4,128)S(1)}, u32[]{:S(2)}) copy-start(f32[10,24,4,128]{3,2,1,0:T(4,128)S(1)} %copy.42) | copy-start | bytes 1474564
  48.7 21.5 %collective-permute-start.4 = (f32[10,24,24,4]{2,1,3,0:T(8,128)}, f32[10,24,24,4]{2,1,3,0:T(8,128)}, u32[]{:S(2)}, u32[]{:S(2)}) collective-permute-start(f32[10,24,24,4]{2,1,3,0:T(8,128)} %copy.43), channel_id=1, source_target_pairs={{0,1},{2,3},{4,5},{6,7},{8,9},{10,11},{12,13},{14,15},{16,17},{18,... | collective-permute-start | bytes 276488 | tf_op jit(solution)/shard_map/ppermute | solution.py:24
  49.9 17.7 %collective-permute-start.5 = (f32[10,24,24,4]{2,1,3,0:T(8,128)}, f32[10,24,24,4]{2,1,3,0:T(8,128)}, u32[]{:S(2)}, u32[]{:S(2)}) collective-permute-start(f32[10,24,24,4]{2,1,3,0:T(8,128)} %copy.44), channel_id=1, source_target_pairs={{1,0},{3,2},{5,4},{7,6},{9,8},{11,10},{13,12},{15,14},{17,16},{19,... | collective-permute-start | bytes 276488 | tf_op jit(solution)/shard_map/ppermute | solution.py:25
  85.1 16.8 %copy-start.30 = (f32[16,16,128]{2,1,0:T(8,128)}, f32[16,16,128]{2,1,0:T(8,128)S(1)}, u32[]{:S(2)}) copy-start(f32[16,16,128]{2,1,0:T(8,128)S(1)} %slice.398) | copy-start | bytes 393220
  104.8 31.1 %copy-start = (f32[8,16,16,128]{3,2,1,0:T(8,128)S(1)}, f32[8,16,16,128]{3,2,1,0:T(8,128)}, u32[]{:S(2)}) copy-start(f32[8,16,16,128]{3,2,1,0:T(8,128)} %fusion.57) | copy-start | bytes 3145732
  105.9 2.6 %collective-permute-start.6 = (f32[8,3,16,128]{3,2,1,0:T(8,128)S(1)}, f32[8,3,16,128]{3,2,1,0:T(8,128)S(1)}, u32[]{:S(2)}, u32[]{:S(2)}) collective-permute-start(f32[8,3,16,128]{3,2,1,0:T(8,128)S(1)} %get-tuple-element.27), channel_id=1, source_target_pairs={{0,32},{32,64},{64,96},{96,128},{128,160},{160,192},{192,224},{1,3... | collective-permute-start | bytes 589832 | tf_op jit(solution)/shard_map/ppermute | solution.py:24
  107.2 8.7 %collective-permute-start.7 = (f32[8,3,16,128]{3,2,1,0:T(8,128)S(1)}, f32[8,3,16,128]{3,2,1,0:T(8,128)S(1)}, u32[]{:S(2)}, u32[]{:S(2)}) collective-permute-start(f32[8,3,16,128]{3,2,1,0:T(8,128)S(1)} %get-tuple-element.28), channel_id=1, source_target_pairs={{32,0},{64,32},{96,64},{128,96},{160,128},{192,160},{224,192},{33,... | collective-permute-start | bytes 589832 | tf_op jit(solution)/shard_map/ppermute | solution.py:25
  115.9 19.2 %copy-start.29 = (f32[8,3,16,128]{3,2,1,0:T(8,128)}, f32[8,3,16,128]{3,2,1,0:T(8,128)S(1)}, u32[]{:S(2)}) copy-start(f32[8,3,16,128]{3,2,1,0:T(8,128)S(1)} %collective-permute-done.7) | copy-start | bytes 589828
  117.4 9.4 %collective-permute-start.9 = (f32[8,22,3,128]{3,0,2,1:T(8,128)S(1)}, f32[8,22,3,128]{3,0,2,1:T(8,128)S(1)}, u32[]{:S(2)}, u32[]{:S(2)}) collective-permute-start(f32[8,22,3,128]{3,0,2,1:T(8,128)S(1)} %copy.48), channel_id=1, source_target_pairs={{2,0},{4,2},{6,4},{8,6},{10,8},{12,10},{14,12},{16,14},{18,16},{20... | collective-permute-start | bytes 811016 | tf_op jit(solution)/shard_map/ppermute | solution.py:25
  119.4 15.7 %collective-permute-start.8 = (f32[8,22,3,128]{3,0,2,1:T(8,128)S(1)}, f32[8,22,3,128]{3,0,2,1:T(8,128)S(1)}, u32[]{:S(2)}, u32[]{:S(2)}) collective-permute-start(f32[8,22,3,128]{3,0,2,1:T(8,128)S(1)} %copy.47), channel_id=1, source_target_pairs={{0,2},{2,4},{4,6},{6,8},{8,10},{10,12},{12,14},{14,16},{16,18},{18... | collective-permute-start | bytes 811016 | tf_op jit(solution)/shard_map/ppermute | solution.py:24
  140.2 25.6 %copy-start.5 = (f32[22,22,134]{2,1,0:T(8,128)S(1)}, f32[22,22,134]{2,1,0:T(8,128)}, u32[]{:S(2)}) copy-start(f32[22,22,134]{2,1,0:T(8,128)} %copy-done.4) | copy-start | bytes 778276
  140.2 25.6 %copy-start.25 = (f32[8,22,3,128]{3,2,1,0:T(4,128)S(1)}, f32[8,22,3,128]{3,2,1,0:T(4,128)}, u32[]{:S(2)}) copy-start(f32[8,22,3,128]{3,2,1,0:T(4,128)} %copy-done.24) | copy-start | bytes 811012
  140.2 25.6 %copy-start.27 = (f32[8,22,3,128]{3,2,1,0:T(4,128)S(1)}, f32[8,22,3,128]{3,2,1,0:T(4,128)}, u32[]{:S(2)}) copy-start(f32[8,22,3,128]{3,2,1,0:T(4,128)} %copy-done.26) | copy-start | bytes 811012
  143.0 20.2 %collective-permute-start.11 = (f32[8,22,22,3]{2,0,3,1:T(8,128)S(1)}, f32[8,22,22,3]{2,0,3,1:T(8,128)S(1)}, u32[]{:S(2)}, u32[]{:S(2)}) collective-permute-start(f32[8,22,22,3]{2,0,3,1:T(8,128)S(1)} %copy.52), channel_id=1, source_target_pairs={{1,0},{3,2},{5,4},{7,6},{9,8},{11,10},{13,12},{15,14},{17,16},{19,... | collective-permute-start | bytes 139400 | tf_op jit(solution)/shard_map/ppermute | solution.py:25
  148.9 11.8 %collective-permute-start.10 = (f32[8,22,22,3]{2,0,3,1:T(8,128)}, f32[8,22,22,3]{2,0,3,1:T(8,128)S(1)}, u32[]{:S(2)}, u32[]{:S(2)}) collective-permute-start(f32[8,22,22,3]{2,0,3,1:T(8,128)} %copy.51), channel_id=1, source_target_pairs={{0,1},{2,3},{4,5},{6,7},{8,9},{10,11},{12,13},{14,15},{16,17},{18,... | collective-permute-start | bytes 139400 | tf_op jit(solution)/shard_map/ppermute | solution.py:24
  (22 other events, 169.1 us)
where the time goes:
time: 252 us; the launch traced here: 248 us
  other arithmetic  74.9 us (30%)
  waiting for transfers between devices  59 us (23%)
  blocking collectives  44.7 us (18%)
  starting transfers between devices  35.7 us (14%)
  local copies, waits for them, and re-layouts  32.2 us (13%)
    psum x5, blocking collectives, over_axes(): shard = lax.psum(shard, axis)  44.7 us
    ppermute x6, waiting for transfers between devices, with_halo(): before = lax.ppermute(last, axis, up)  31.5 us
    mul x3, other arithmetic, shards(): flux = trim_to(conduct_wide, outer - margin) * adjoint  29 us
    ppermute x6, waiting for transfers between devices, with_halo(): after = lax.ppermute(leading, axis, down)  27.5 us
    ppermute x6, starting transfers between devices, with_halo(): after = lax.ppermute(leading, axis, down)  21.1 us
    add x2, other arithmetic, shards(): inner + cheb_w[step] * (trim_to(source_wide, cut) - applied) / diag_here  14.8 us
    ppermute x6, starting transfers between devices, with_halo(): before = lax.ppermute(last, axis, up)  14.6 us
    concatenate x3, other arithmetic, with_halo(): shard = jnp.concatenate([before, shard, after], axis=dim)  9.32 us
  transfers between devices with their start and end apart: 12, of which 8 were waited for; matrix products, arithmetic and copies ran while one was open for 3% of the time, Pallas kernels for 0%

commit v1 on v0

--- a/solution.py
+++ b/solution.py
@@ -29,7 +29,8 @@
 
 def over_axes(shard, axes):
     for axis in axes:
-        shard = lax.psum(shard, axis)
+        parts = lax.all_gather(shard, axis, axis=0, tiled=False)
+        shard = parts.sum(axis=0)
     return shard
 
 

time: 252 us -> 254 us (level)
  waiting for transfers between devices: 59 us -> 52.7 us
  local copies, waits for them, and re-layouts: 32.2 us -> 36.8 us
  between operations: 1.51 us -> 4.82 us
    psum x5 -> x0, blocking collectives: 44.7 us -> none  [over_axes(): shard = lax.psum(shard, axis)]
    unnamed x0 -> x5, blocking collectives: none -> 44.6 us
    unnamed x68 -> x93, local copies, waits for them, and re-layouts: 1.66 us -> 5.78 us
    ppermute x6, waiting for transfers between devices: 31.5 us -> 27.8 us  [with_halo(): before = lax.ppermute(last, axis, up)]
    ppermute x6, waiting for transfers between devices: 27.5 us -> 24.9 us  [with_halo(): after = lax.ppermute(leading, axis, down)]
  transfers between devices with their start and end apart: 12 -> 12, of which waited for: 8 -> 7; matrix products, arithmetic and copies ran while one was open for 3% -> 5% of each run, Pallas kernels for 0% -> 0%
where the time goes in v1:
time: 254 us; the launch traced here: 250 us
  other arithmetic  75 us (30%)
  waiting for transfers between devices  52.7 us (21%)
  blocking collectives  44.6 us (18%)
  local copies, waits for them, and re-layouts  36.8 us (14%)
  starting transfers between devices  35.7 us (14%)
  between operations  4.82 us (2%)
    unnamed x5, blocking collectives  44.6 us
    mul x3, other arithmetic, shards(): flux = trim_to(conduct_wide, outer - margin) * adjoint  28.9 us
    ppermute x6, waiting for transfers between devices, with_halo(): before = lax.ppermute(last, axis, up)  27.8 us
    ppermute x6, waiting for transfers between devices, with_halo(): after = lax.ppermute(leading, axis, down)  24.9 us
    ppermute x6, starting transfers between devices, with_halo(): after = lax.ppermute(leading, axis, down)  21.1 us
    add x2, other arithmetic, shards(): inner + cheb_w[step] * (trim_to(source_wide, cut) - applied) / diag_here  14.8 us
    ppermute x6, starting transfers between devices, with_halo(): before = lax.ppermute(last, axis, up)  14.6 us
    concatenate x3, other arithmetic, with_halo(): shard = jnp.concatenate([before, shard, after], axis=dim)  9.32 us
  transfers between devices with their start and end apart: 12, of which 7 were waited for; matrix products, arithmetic and copies ran while one was open for 5% of the time, Pallas kernels for 0%

profile of v1, /device:TPU:6, one launch (start us, length us, event | category | flops | bytes accessed | tf_op | source)
XLA Modules:
  0.0 249.7 jit_solution(10377951148598307721)
XLA Ops:
  6.0 3.5 %collective-permute-done.1 = f32[10,4,16,128]{3,2,1,0:T(8,128)S(1)} collective-permute-done((f32[10,4,16,128]{3,2,1,0:T(8,128)S(1)}, f32[10,4,16,128]{3,2,1,0:T(8,128)S(1)}, u32[]{:S(2)}, u32[]{:S(2)}) %collective-permute-start.1) | collective-permute-done | bytes 327712 | tf_op jit(solution)/shard_map/ppermute | solution.py:25
  13.9 4.0 %collective-permute-start.2 = (f32[10,24,4,128]{3,1,2,0:T(8,128)S(1)}, f32[10,24,4,128]{3,1,2,0:T(8,128)S(1)}, u32[]{:S(2)}, u32[]{:S(2)}) collective-permute-start(f32[10,24,4,128]{3,1,2,0:T(8,128)S(1)} %copy.39), channel_id=1, source_target_pairs={{0,2},{2,4},{4,6},{6,8},{8,10},{10,12},{12,14},{14,16},{16,18},{18... | collective-permute-start | bytes 1474568 | tf_op jit(solution)/shard_map/ppermute | solution.py:24
  17.9 5.8 %collective-permute-done.3 = f32[10,24,4,128]{3,1,2,0:T(8,128)S(1)} collective-permute-done((f32[10,24,4,128]{3,1,2,0:T(8,128)S(1)}, f32[10,24,4,128]{3,1,2,0:T(8,128)S(1)}, u32[]{:S(2)}, u32[]{:S(2)}) %collective-permute-start.3) | collective-permute-done | bytes 491552 | tf_op jit(solution)/shard_map/ppermute | solution.py:25
  23.9 14.6 %collective-permute-done.2 = f32[10,24,4,128]{3,1,2,0:T(8,128)S(1)} collective-permute-done((f32[10,24,4,128]{3,1,2,0:T(8,128)S(1)}, f32[10,24,4,128]{3,1,2,0:T(8,128)S(1)}, u32[]{:S(2)}, u32[]{:S(2)}) %collective-permute-start.2) | collective-permute-done | bytes 491552 | tf_op jit(solution)/shard_map/ppermute | solution.py:24
  42.5 3.7 %copy.44 = f32[10,24,24,4]{2,1,3,0:T(8,128)} copy(f32[10,24,24,4]{3,2,1,0:T(8,128)} %get-tuple-element.17) | data formatting | bytes 184320 | tf_op jit(solution)/shard_map/slice | solution.py:23
  49.9 8.0 %collective-permute-start.5 = (f32[10,24,24,4]{2,1,3,0:T(8,128)}, f32[10,24,24,4]{2,1,3,0:T(8,128)}, u32[]{:S(2)}, u32[]{:S(2)}) collective-permute-start(f32[10,24,24,4]{2,1,3,0:T(8,128)} %copy.44), channel_id=1, source_target_pairs={{1,0},{3,2},{5,4},{7,6},{9,8},{11,10},{13,12},{15,14},{17,16},{19,... | collective-permute-start | bytes 276488 | tf_op jit(solution)/shard_map/ppermute | solution.py:25
  59.5 8.1 %collective-permute-done.5 = f32[10,24,24,4]{2,1,3,0:T(8,128)} collective-permute-done((f32[10,24,24,4]{2,1,3,0:T(8,128)}, f32[10,24,24,4]{2,1,3,0:T(8,128)}, u32[]{:S(2)}, u32[]{:S(2)}) %collective-permute-start.5) | collective-permute-done | bytes 92192 | tf_op jit(solution)/shard_map/ppermute | solution.py:25
  70.1 3.9 %copy.45 = f32[10,24,24,4]{3,2,1,0:T(8,128)} copy(f32[10,24,24,4]{2,1,3,0:T(8,128)} %collective-permute-done.4) | data formatting | bytes 184320 | tf_op jit(solution)/shard_map/ppermute | solution.py:24
  74.1 8.5 %pad_maximum_fusion = f32[10,24,24,136]{3,2,1,0:T(8,128)S(1)} fusion(f32[10,24,24,4]{3,2,1,0:T(8,128)S(1)} %copy.46, f32[10,24,4,128]{3,2,1,0:T(4,128)S(1)} %copy.42, f32[10,4,16,128]{3,2,1,0:T(8,128)} %copy-done.12, f32[8,16,16,128]{3,2,1,0:T(8,128)} %param.4, f32[1,16,16,128]{3,2,1,0:T(8,128)} %copy-done.14, f32[1,16,16,128]{3,2,1,0:T(8,128)} %bitcast.14, ...), kind=kLoop, calls=%fused_computation | loop fusion | flops 6266880 | bytes 6266880 | tf_op jit(solution)/shard_map/concatenate | solution.py:26
  87.1 7.5 %fusion.11 = f32[8,20,20,132]{3,2,1,0:T(8,128)S(1)} fusion(f32[8,22,22,134]{3,2,1,0:T(8,128)S(1)} %get-tuple-element.13, f32[8,22,22,134]{3,2,1,0:T(8,128)S(1)} %get-tuple-element.14, f32[20,20,132]{2,1,0:T(8,128)S(1)} %slice.379, f32[20,20,132]{2,1,0:T(8,128)S(1)} %slice.378), kind=kLoop, calls=%fused_computation.26 | loop fusion | flops 5068800 | bytes 15628800 | tf_op jit(solution)/shard_map/add | solution.py:81
  94.6 7.3 %fusion.22 = f32[8,18,18,130]{3,2,1,0:T(8,128)S(1)} fusion(f32[8,20,20,132]{3,2,1,0:T(8,128)S(1)} %fusion.11, f32[8,22,22,134]{3,2,1,0:T(8,128)S(1)} %get-tuple-element.14, f32[18,18,130]{2,1,0:T(8,128)S(1)} %slice.389, f32[18,18,130]{2,1,0:T(8,128)S(1)} %slice.388), kind=kLoop, calls=%fused_computation.47 | loop fusion | flops 4043520 | bytes 12467520 | tf_op jit(solution)/shard_map/add | solution.py:81
  108.7 7.4 %collective-permute-done.7 = f32[8,3,16,128]{3,2,1,0:T(8,128)S(1)} collective-permute-done((f32[8,3,16,128]{3,2,1,0:T(8,128)S(1)}, f32[8,3,16,128]{3,2,1,0:T(8,128)S(1)}, u32[]{:S(2)}, u32[]{:S(2)}) %collective-permute-start.7) | collective-permute-done | bytes 196640 | tf_op jit(solution)/shard_map/ppermute | solution.py:25
  119.5 4.8 %collective-permute-start.8 = (f32[8,22,3,128]{3,0,2,1:T(8,128)S(1)}, f32[8,22,3,128]{3,0,2,1:T(8,128)S(1)}, u32[]{:S(2)}, u32[]{:S(2)}) collective-permute-start(f32[8,22,3,128]{3,0,2,1:T(8,128)S(1)} %copy.47), channel_id=1, source_target_pairs={{0,2},{2,4},{4,6},{6,8},{8,10},{10,12},{12,14},{14,16},{16,18},{18... | collective-permute-start | bytes 811016 | tf_op jit(solution)/shard_map/ppermute | solution.py:24
  130.7 4.5 %collective-permute-done.8 = f32[8,22,3,128]{3,0,2,1:T(8,128)S(1)} collective-permute-done((f32[8,22,3,128]{3,0,2,1:T(8,128)S(1)}, f32[8,22,3,128]{3,0,2,1:T(8,128)S(1)}, u32[]{:S(2)}, u32[]{:S(2)}) %collective-permute-start.8) | collective-permute-done | bytes 270368 | tf_op jit(solution)/shard_map/ppermute | solution.py:24
  143.2 5.9 %collective-permute-start.11 = (f32[8,22,22,3]{2,0,3,1:T(8,128)S(1)}, f32[8,22,22,3]{2,0,3,1:T(8,128)S(1)}, u32[]{:S(2)}, u32[]{:S(2)}) collective-permute-start(f32[8,22,22,3]{2,0,3,1:T(8,128)S(1)} %copy.52), channel_id=1, source_target_pairs={{1,0},{3,2},{5,4},{7,6},{9,8},{11,10},{13,12},{15,14},{17,16},{19,... | collective-permute-start | bytes 139400 | tf_op jit(solution)/shard_map/ppermute | solution.py:25
  152.2 8.7 %collective-permute-done.10 = f32[8,22,22,3]{2,0,3,1:T(8,128)S(1)} collective-permute-done((f32[8,22,22,3]{2,0,3,1:T(8,128)}, f32[8,22,22,3]{2,0,3,1:T(8,128)S(1)}, u32[]{:S(2)}, u32[]{:S(2)}) %collective-permute-start.10) | collective-permute-done | bytes 46496 | tf_op jit(solution)/shard_map/ppermute | solution.py:24
  165.9 8.0 %broadcast_multiply_fusion = (f32[8,22,22,134]{3,2,1,0:T(8,128)S(1)}, f32[8,22,22,134]{3,2,1,0:T(8,128)}, f32[8,22,22,134]{3,2,1,0:T(8,128)S(1)}) fusion(f32[22,22,134]{2,1,0:T(8,128)} %get-tuple-element.29, f32[22,22,134]{2,1,0:T(8,128)S(1)} %copy-done.5, f32[8,22,22,3]{3,2,1,0:T(8,128)} %copy.54, f32[8,22,3,128]{3,2,1,0:T(4,128)S(1)} %copy-done.25, ...), kind=kLoop, calls=%fused_computation.54 | loop fusion | flops 4669632 | bytes 8820416 | tf_op jit(solution)/shard_map/mul | solution.py:87
  173.9 10.7 %broadcast_multiply_fusion.1 = (f32[8,20,20,132]{3,2,1,0:T(8,128)S(1)}, f32[8,20,20,132]{3,2,1,0:T(8,128)}) fusion(f32[20,20,132]{2,1,0:T(8,128)S(1)} %copy-done.17, f32[8,22,22,134]{3,2,1,0:T(8,128)S(1)} %get-tuple-element.10, f32[20,20,132]{2,1,0:T(8,128)S(1)} %copy-done.19, f32[8,22,22,134]{3,2,1,0:T(8,128)S(1)} %get-tuple-element.12, ...), kind=kLoop, calls=%fused_computation.55 | loop fusion | flops 5068800 | bytes 17318400 | tf_op jit(solution)/shard_map/mul | solution.py:87
  184.6 10.3 %broadcast_multiply_fusion.2 = (f32[8,18,18,130]{3,2,1,0:T(8,128)S(1)}, f32[8,18,18,130]{3,2,1,0:T(8,128)}) fusion(f32[18,18,130]{2,1,0:T(8,128)} %copy-done.20, f32[8,20,20,132]{3,2,1,0:T(8,128)S(1)} %get-tuple-element.8, f32[18,18,130]{2,1,0:T(8,128)} %copy-done.21, f32[8,22,22,134]{3,2,1,0:T(8,128)S(1)} %get-tuple-element.12, ...), kind=kLoop, calls=%fused_computation.56 | loop fusion | flops 4043520 | bytes 13815360 | tf_op jit(solution)/shard_map/mul | solution.py:87
  195.0 7.7 %multiply_reduce_fusion = (f32[8]{0:T(128)S(1)}, f32[8,16,16,128]{3,2,1,0:T(8,128)}) fusion(f32[8,16,16,128]{3,2,1,0:T(8,128)S(1)} %copy-done.3, f32[10,24,4,128]{3,2,1,0:T(4,128)S(1)} %copy-done.7, f32[10,4,16,128]{3,2,1,0:T(8,128)S(1)} %copy-done.13, f32[1,16,16,128]{3,2,1,0:T(8,128)S(1)} %copy-done.15, f32[1,16,16,128]{3,2,1,0:T(8,128)S(1)} %bitcast.16, ...), kind=kLoop, calls=%fused_computation.117 | loop fusion | flops 13893624 | bytes 12832800 | tf_op jit(solution)/shard_map/reduce_sum | solution.py:107
  202.8 11.8 %all-reduce = f32[32]{0:T(128)S(1)} all-reduce(f32[32]{0:T(128)S(1)} %dynamic-update-slice), channel_id=2, replica_groups=mesh['gx_0'=4,'gx_1'=2,'gy_0'=8,'gy_1'=2,'gz'=2] {'gx_0'}, use_global_device_ids=true, to_apply=%add | all-reduce | flops 32 | bytes 256
  217.8 19.1 %all-reduce.2 = f32[64]{0:T(128)S(1)} all-reduce(f32[64]{0:T(128)S(1)} %dynamic-update-slice.2), channel_id=4, replica_groups=mesh['gx_0'=4,'gx_1'=2,'gy_0'=8,'gy_1'=2,'gz'=2] {'gy_0'}, use_global_device_ids=true, to_apply=%add.2 | all-reduce | flops 64 | bytes 512
  237.2 4.9 %all-reduce.3 = f32[16]{0:T(128)S(1)} all-reduce(f32[16]{0:T(128)S(1)} %dynamic-update-slice.3), channel_id=5, replica_groups=mesh['gx_0'=4,'gx_1'=2,'gy_0'=8,'gy_1'=2,'gz'=2] {'gy_1'}, use_global_device_ids=true, to_apply=%add.3 | all-reduce | flops 16 | bytes 128
  242.5 6.4 %all-reduce.4 = f32[16]{0:T(128)S(1)} all-reduce(f32[16]{0:T(128)S(1)} %dynamic-update-slice.4), channel_id=6, replica_groups=mesh['gx_0'=4,'gx_1'=2,'gy_0'=8,'gy_1'=2,'gz'=2] {'gz'}, use_global_device_ids=true, to_apply=%add.4 | all-reduce | flops 16 | bytes 128
  (153 shorter events, 59.8 us)
Async XLA Ops:
  1.6 37.0 %copy-start.14 = (f32[1,16,16,128]{3,2,1,0:T(8,128)}, f32[1,16,16,128]{3,2,1,0:T(8,128)S(1)}, u32[]{:S(2)}) copy-start(f32[1,16,16,128]{3,2,1,0:T(8,128)S(1)} %exponential_bitcast_fusion) | copy-start | bytes 393220
  2.7 36.6 %copy-start.2 = (f32[8,16,16,128]{3,2,1,0:T(8,128)S(1)}, f32[8,16,16,128]{3,2,1,0:T(8,128)}, u32[]{:S(2)}) copy-start(f32[8,16,16,128]{3,2,1,0:T(8,128)} %param.4) | copy-start | bytes 3145732
  2.7 36.6 %copy-start.22 = (f32[16,16,128]{2,1,0:T(8,128)S(1)}, f32[16,16,128]{2,1,0:T(8,128)}, u32[]{:S(2)}) copy-start(f32[16,16,128]{2,1,0:T(8,128)} %param.5) | copy-start | bytes 393220
  2.7 3.2 %collective-permute-start = (f32[10,4,16,128]{3,2,1,0:T(8,128)S(1)}, f32[10,4,16,128]{3,2,1,0:T(8,128)S(1)}, u32[]{:S(2)}, u32[]{:S(2)}) collective-permute-start(f32[10,4,16,128]{3,2,1,0:T(8,128)S(1)} %get-tuple-element.25), channel_id=1, source_target_pairs={{0,32},{32,64},{64,96},{96,128},{128,160},{160,192},{192,224},{1,3... | collective-permute-start | bytes 983048 | tf_op jit(solution)/shard_map/ppermute | solution.py:24
  4.6 4.9 %collective-permute-start.1 = (f32[10,4,16,128]{3,2,1,0:T(8,128)S(1)}, f32[10,4,16,128]{3,2,1,0:T(8,128)S(1)}, u32[]{:S(2)}, u32[]{:S(2)}) collective-permute-start(f32[10,4,16,128]{3,2,1,0:T(8,128)S(1)} %get-tuple-element.26), channel_id=1, source_target_pairs={{32,0},{64,32},{96,64},{128,96},{160,128},{192,160},{224,192},{33,... | collective-permute-start | bytes 983048 | tf_op jit(solution)/shard_map/ppermute | solution.py:25
  5.9 33.9 %copy-start.10 = (f32[10,4,16,128]{3,2,1,0:T(8,128)}, f32[10,4,16,128]{3,2,1,0:T(8,128)S(1)}, u32[]{:S(2)}) copy-start(f32[10,4,16,128]{3,2,1,0:T(8,128)S(1)} %collective-permute-done) | copy-start | bytes 983044
  9.5 30.3 %copy-start.12 = (f32[10,4,16,128]{3,2,1,0:T(8,128)}, f32[10,4,16,128]{3,2,1,0:T(8,128)S(1)}, u32[]{:S(2)}) copy-start(f32[10,4,16,128]{3,2,1,0:T(8,128)S(1)} %collective-permute-done.1) | copy-start | bytes 983044
  11.1 12.6 %collective-permute-start.3 = (f32[10,24,4,128]{3,1,2,0:T(8,128)S(1)}, f32[10,24,4,128]{3,1,2,0:T(8,128)S(1)}, u32[]{:S(2)}, u32[]{:S(2)}) collective-permute-start(f32[10,24,4,128]{3,1,2,0:T(8,128)S(1)} %copy.40), channel_id=1, source_target_pairs={{2,0},{4,2},{6,4},{8,6},{10,8},{12,10},{14,12},{16,14},{18,16},{20... | collective-permute-start | bytes 1474568 | tf_op jit(solution)/shard_map/ppermute | solution.py:25
  13.9 24.5 %collective-permute-start.2 = (f32[10,24,4,128]{3,1,2,0:T(8,128)S(1)}, f32[10,24,4,128]{3,1,2,0:T(8,128)S(1)}, u32[]{:S(2)}, u32[]{:S(2)}) collective-permute-start(f32[10,24,4,128]{3,1,2,0:T(8,128)S(1)} %copy.39), channel_id=1, source_target_pairs={{0,2},{2,4},{4,6},{6,8},{8,10},{10,12},{12,14},{14,16},{16,18},{18... | collective-permute-start | bytes 1474568 | tf_op jit(solution)/shard_map/ppermute | solution.py:24
  23.9 50.2 %copy-start.6 = (f32[10,24,4,128]{3,2,1,0:T(4,128)}, f32[10,24,4,128]{3,2,1,0:T(4,128)S(1)}, u32[]{:S(2)}) copy-start(f32[10,24,4,128]{3,2,1,0:T(4,128)S(1)} %copy.42) | copy-start | bytes 1474564
  48.7 21.5 %collective-permute-start.4 = (f32[10,24,24,4]{2,1,3,0:T(8,128)}, f32[10,24,24,4]{2,1,3,0:T(8,128)}, u32[]{:S(2)}, u32[]{:S(2)}) collective-permute-start(f32[10,24,24,4]{2,1,3,0:T(8,128)} %copy.43), channel_id=1, source_target_pairs={{0,1},{2,3},{4,5},{6,7},{8,9},{10,11},{12,13},{14,15},{16,17},{18,... | collective-permute-start | bytes 276488 | tf_op jit(solution)/shard_map/ppermute | solution.py:24
  49.9 17.7 %collective-permute-start.5 = (f32[10,24,24,4]{2,1,3,0:T(8,128)}, f32[10,24,24,4]{2,1,3,0:T(8,128)}, u32[]{:S(2)}, u32[]{:S(2)}) collective-permute-start(f32[10,24,24,4]{2,1,3,0:T(8,128)} %copy.44), channel_id=1, source_target_pairs={{1,0},{3,2},{5,4},{7,6},{9,8},{11,10},{13,12},{15,14},{17,16},{19,... | collective-permute-start | bytes 276488 | tf_op jit(solution)/shard_map/ppermute | solution.py:25
  104.9 23.2 %copy-start.35 = (u32[256]{0:T(256)S(1)}, u32[256]{0:T(256)}, u32[]{:S(2)}) copy-start(u32[256]{0:T(256)} %constant.29) | copy-start | bytes 3076
  104.9 24.5 %copy-start.34 = (u32[256]{0:T(256)S(1)}, u32[256]{0:T(256)}, u32[]{:S(2)}) copy-start(u32[256]{0:T(256)} %constant.24) | copy-start | bytes 3076
  104.9 31.2 %copy-start = (f32[8,16,16,128]{3,2,1,0:T(8,128)S(1)}, f32[8,16,16,128]{3,2,1,0:T(8,128)}, u32[]{:S(2)}) copy-start(f32[8,16,16,128]{3,2,1,0:T(8,128)} %fusion.57) | copy-start | bytes 3145732
  106.0 2.6 %collective-permute-start.6 = (f32[8,3,16,128]{3,2,1,0:T(8,128)S(1)}, f32[8,3,16,128]{3,2,1,0:T(8,128)S(1)}, u32[]{:S(2)}, u32[]{:S(2)}) collective-permute-start(f32[8,3,16,128]{3,2,1,0:T(8,128)S(1)} %get-tuple-element.27), channel_id=1, source_target_pairs={{0,32},{32,64},{64,96},{96,128},{128,160},{160,192},{192,224},{1,3... | collective-permute-start | bytes 589832 | tf_op jit(solution)/shard_map/ppermute | solution.py:24
  107.3 8.7 %collective-permute-start.7 = (f32[8,3,16,128]{3,2,1,0:T(8,128)S(1)}, f32[8,3,16,128]{3,2,1,0:T(8,128)S(1)}, u32[]{:S(2)}, u32[]{:S(2)}) collective-permute-start(f32[8,3,16,128]{3,2,1,0:T(8,128)S(1)} %get-tuple-element.28), channel_id=1, source_target_pairs={{32,0},{64,32},{96,64},{128,96},{160,128},{192,160},{224,192},{33,... | collective-permute-start | bytes 589832 | tf_op jit(solution)/shard_map/ppermute | solution.py:25
  117.5 13.0 %collective-permute-start.9 = (f32[8,22,3,128]{3,0,2,1:T(8,128)S(1)}, f32[8,22,3,128]{3,0,2,1:T(8,128)S(1)}, u32[]{:S(2)}, u32[]{:S(2)}) collective-permute-start(f32[8,22,3,128]{3,0,2,1:T(8,128)S(1)} %copy.48), channel_id=1, source_target_pairs={{2,0},{4,2},{6,4},{8,6},{10,8},{12,10},{14,12},{16,14},{18,16},{20... | collective-permute-start | bytes 811016 | tf_op jit(solution)/shard_map/ppermute | solution.py:25
  119.5 15.7 %collective-permute-start.8 = (f32[8,22,3,128]{3,0,2,1:T(8,128)S(1)}, f32[8,22,3,128]{3,0,2,1:T(8,128)S(1)}, u32[]{:S(2)}, u32[]{:S(2)}) collective-permute-start(f32[8,22,3,128]{3,0,2,1:T(8,128)S(1)} %copy.47), channel_id=1, source_target_pairs={{0,2},{2,4},{4,6},{6,8},{8,10},{10,12},{12,14},{14,16},{16,18},{18... | collective-permute-start | bytes 811016 | tf_op jit(solution)/shard_map/ppermute | solution.py:24
  140.3 25.6 %copy-start.5 = (f32[22,22,134]{2,1,0:T(8,128)S(1)}, f32[22,22,134]{2,1,0:T(8,128)}, u32[]{:S(2)}) copy-start(f32[22,22,134]{2,1,0:T(8,128)} %copy-done.4) | copy-start | bytes 778276
  140.3 25.6 %copy-start.25 = (f32[8,22,3,128]{3,2,1,0:T(4,128)S(1)}, f32[8,22,3,128]{3,2,1,0:T(4,128)}, u32[]{:S(2)}) copy-start(f32[8,22,3,128]{3,2,1,0:T(4,128)} %copy-done.24) | copy-start | bytes 811012
  140.3 25.6 %copy-start.27 = (f32[8,22,3,128]{3,2,1,0:T(4,128)S(1)}, f32[8,22,3,128]{3,2,1,0:T(4,128)}, u32[]{:S(2)}) copy-start(f32[8,22,3,128]{3,2,1,0:T(4,128)} %copy-done.26) | copy-start | bytes 811012
  143.2 20.2 %collective-permute-start.11 = (f32[8,22,22,3]{2,0,3,1:T(8,128)S(1)}, f32[8,22,22,3]{2,0,3,1:T(8,128)S(1)}, u32[]{:S(2)}, u32[]{:S(2)}) collective-permute-start(f32[8,22,22,3]{2,0,3,1:T(8,128)S(1)} %copy.52), channel_id=1, source_target_pairs={{1,0},{3,2},{5,4},{7,6},{9,8},{11,10},{13,12},{15,14},{17,16},{19,... | collective-permute-start | bytes 139400 | tf_op jit(solution)/shard_map/ppermute | solution.py:25
  149.1 11.8 %collective-permute-start.10 = (f32[8,22,22,3]{2,0,3,1:T(8,128)}, f32[8,22,22,3]{2,0,3,1:T(8,128)S(1)}, u32[]{:S(2)}, u32[]{:S(2)}) collective-permute-start(f32[8,22,22,3]{2,0,3,1:T(8,128)} %copy.51), channel_id=1, source_target_pairs={{0,1},{2,3},{4,5},{6,7},{8,9},{10,11},{12,13},{14,15},{16,17},{18,... | collective-permute-start | bytes 139400 | tf_op jit(solution)/shard_map/ppermute | solution.py:24
  (27 other events, 262.8 us)
